TPU v7x, 32 devices: a whole 2x2x4 slice. The times are simulated.
32 devices in a mesh: grp: 8 (over z, y), blk: 4 (over x, core).
Axes of the slice: x: 2, y: 2, z: 4, core: 2. Of those that a mesh axis runs over, the one named last changes fastest.
Arguments:
- query: bfloat16 [4096, 512], P(('grp', 'blk')), may hold values from -6 to 6
- key: bfloat16 [4096, 512], P(('grp', 'blk')), may hold values from -6 to 6
- value: bfloat16 [4096, 512], P(('grp', 'blk')), may hold values from -6 to 6
- gate_u: bfloat16 [4096, 512], P(('grp', 'blk')), may hold values from -6 to 6
- out_grad: bfloat16 [4096, 1024], P(('grp', 'blk')), may hold values from -6 to 6
- lengths: int32 [8], P('grp'), may hold values from 32 to 512
- norm_gain: float32 [512], replicated, may hold values from 0.1 to 1.9
- out_weight: bfloat16 [512, 1024], replicated, may hold values from -0.25 to 0.25
Outputs:
- layer_out: bfloat16 [4096, 1024], P(('grp', 'blk'))
- grad_query: bfloat16 [4096, 512], P(('grp', 'blk'))
- grad_key: bfloat16 [4096, 512], P(('grp', 'blk'))
- grad_value: bfloat16 [4096, 512], P(('grp', 'blk'))
- grad_gate: bfloat16 [4096, 512], P(('grp', 'blk'))
- grad_weight: float32 [512, 1024], P(None, 'blk')
Inputs may be any that keep to these rules, and one draw needn't show every extreme that they name: `lengths`: events of a user at or past its length are padding.
All inputs are finite; a program needn't handle non-finite values.
Results may differ from a plain program's by a relative error of at most 0.009.
Values may be sent and summed in bfloat16 or wider, within the bound.
No kernel may reach another device: no remote copies, remote signals or barrier semaphores. Data moves between devices by JAX's collectives and lax.ppermute only.
A program may use at most 64 MiB of HBM per device.

v0:
```python
import math
import jax
import jax.numpy as jnp
from jax import lax
from jax.sharding import PartitionSpec as P

HEADS = 8
HEAD = 64
EPS = 1e-05


def causal_mask(query_pos, key_pos, length):
    return (
        (key_pos[None, :] <= query_pos[:, None])
        & (query_pos[:, None] < length)
        & (key_pos[None, :] < length)
    )


def over_blocks(total_rows, step_fn, initial):
    size = math.gcd(total_rows, 512)

    def advance(index, carry):
        return step_fn(carry, index * size, size)

    return lax.fori_loop(0, total_rows // size, advance, initial)


def shards(query, key, value, gate_u, out_grad, lengths, norm_gain, out_weight):
    rows = query.shape[0]
    scale = HEAD ** (-0.5)
    length = lengths[0]
    lanes = lax.axis_size("blk")
    position = lax.axis_index("blk")
    first_row = position * rows
    row_pos = first_row + jnp.arange(rows, dtype=jnp.int32)
    total_len = rows * lanes
    query_heads = query.reshape(rows, HEADS, HEAD)
    key_heads = key.reshape(rows, HEADS, HEAD)
    value_heads = value.reshape(rows, HEADS, HEAD)
    zeros = jnp.zeros((rows, HEADS, HEAD), jnp.float32)
    keys_all, values_all = (
        lax.all_gather(key, "blk", axis=0, tiled=True),
        lax.all_gather(value, "blk", axis=0, tiled=True),
    )

    def forward_step(carry, begin, size):
        key_block = lax.dynamic_slice_in_dim(keys_all, begin, size, 0).reshape(size, HEADS, HEAD)
        value_block = lax.dynamic_slice_in_dim(values_all, begin, size, 0).reshape(
            size, HEADS, HEAD
        )
        scores = (
            jnp.einsum("rhd,nhd->hrn", query_heads, key_block, preferred_element_type=jnp.float32)
            * scale
        )
        mask = causal_mask(row_pos, begin + jnp.arange(size, dtype=jnp.int32), length)
        weights = (jax.nn.silu(scores) * mask[None]).astype(jnp.bfloat16)
        return carry + jnp.einsum(
            "hrn,nhd->rhd", weights, value_block, preferred_element_type=jnp.float32
        )

    attended = over_blocks(total_len, forward_step, zeros).reshape(rows, HEADS * HEAD)
    centre = attended - jnp.mean(attended, axis=1, keepdims=True)
    inv_std = lax.rsqrt(jnp.mean(centre * centre, axis=1, keepdims=True) + EPS)
    normed = centre * inv_std
    scaled = normed * norm_gain
    gates = gate_u.astype(jnp.float32)
    mixed = (scaled * gates).astype(jnp.bfloat16)
    layer_out = jnp.dot(mixed, out_weight, preferred_element_type=jnp.float32).astype(jnp.bfloat16)
    mixed_grad = lax.dot_general(
        out_grad, out_weight, (((1,), (1,)), ((), ())), preferred_element_type=jnp.float32
    )
    grad_gate = (mixed_grad * scaled).astype(jnp.bfloat16)
    normed_grad = mixed_grad * gates * norm_gain
    attended_grad = inv_std * (
        normed_grad
        - jnp.mean(normed_grad, axis=1, keepdims=True)
        - normed * jnp.mean(normed_grad * normed, axis=1, keepdims=True)
    )
    attended_grad = attended_grad.astype(jnp.bfloat16)
    grad_heads = attended_grad.reshape(rows, HEADS, HEAD)
    weight_term = lax.dot_general(
        mixed, out_grad, (((0,), (0,)), ((), ())), preferred_element_type=jnp.float32
    )

    def query_step(carry, begin, size):
        key_block = lax.dynamic_slice_in_dim(keys_all, begin, size, 0).reshape(size, HEADS, HEAD)
        value_block = lax.dynamic_slice_in_dim(values_all, begin, size, 0).reshape(
            size, HEADS, HEAD
        )
        scores = (
            jnp.einsum("rhd,nhd->hrn", query_heads, key_block, preferred_element_type=jnp.float32)
            * scale
        )
        mask = causal_mask(row_pos, begin + jnp.arange(size, dtype=jnp.int32), length)
        sigma = jax.nn.sigmoid(scores)
        prob_grad = jnp.einsum(
            "rhd,nhd->hrn", grad_heads, value_block, preferred_element_type=jnp.float32
        )
        score_grad = (prob_grad * sigma * (1.0 + scores * (1.0 - sigma)) * mask[None]).astype(
            jnp.bfloat16
        )
        return carry + jnp.einsum(
            "hrn,nhd->rhd", score_grad, key_block, preferred_element_type=jnp.float32
        )

    grad_query = (
        (over_blocks(total_len, query_step, zeros) * scale)
        .reshape(rows, HEADS * HEAD)
        .astype(jnp.bfloat16)
    )
    query_piece = lax.all_gather(query, "blk", axis=0, tiled=True)
    grad_piece = lax.all_gather(attended_grad, "blk", axis=0, tiled=True)
    count = query_piece.shape[0]

    def inner(acc, begin, size):
        key_acc, value_acc = acc
        query_block = lax.dynamic_slice_in_dim(query_piece, begin, size, 0).reshape(
            size, HEADS, HEAD
        )
        grad_block = lax.dynamic_slice_in_dim(grad_piece, begin, size, 0).reshape(size, HEADS, HEAD)
        scores = (
            jnp.einsum("nhd,rhd->hnr", query_block, key_heads, preferred_element_type=jnp.float32)
            * scale
        )
        mask = causal_mask(begin + jnp.arange(size, dtype=jnp.int32), row_pos, length)
        weights = (jax.nn.silu(scores) * mask[None]).astype(jnp.bfloat16)
        sigma = jax.nn.sigmoid(scores)
        prob_grad = jnp.einsum(
            "nhd,rhd->hnr", grad_block, value_heads, preferred_element_type=jnp.float32
        )
        score_grad = (prob_grad * sigma * (1.0 + scores * (1.0 - sigma)) * mask[None]).astype(
            jnp.bfloat16
        )
        key_acc = key_acc + jnp.einsum(
            "hnr,nhd->rhd", score_grad, query_block, preferred_element_type=jnp.float32
        )
        value_acc = value_acc + jnp.einsum(
            "hnr,nhd->rhd", weights, grad_block, preferred_element_type=jnp.float32
        )
        return (key_acc, value_acc)

    key_acc, value_acc = over_blocks(count, inner, (zeros, zeros))
    grad_key = (key_acc * scale).reshape(rows, HEADS * HEAD).astype(jnp.bfloat16)
    grad_value = value_acc.reshape(rows, HEADS * HEAD).astype(jnp.bfloat16)
    column_part = lax.psum_scatter(weight_term, "blk", scatter_dimension=1, tiled=True)
    grad_weight = lax.psum(column_part, "grp")
    return (layer_out, grad_query, grad_key, grad_value, grad_gate, grad_weight)


def solution(mesh):
    return jax.shard_map(
        shards,
        mesh=mesh,
        in_specs=(
            P(("grp", "blk"), None),
            P(("grp", "blk"), None),
            P(("grp", "blk"), None),
            P(("grp", "blk"), None),
            P(("grp", "blk"), None),
            P("grp"),
            P(),
            P(),
        ),
        out_specs=(
            P(("grp", "blk"), None),
            P(("grp", "blk"), None),
            P(("grp", "blk"), None),
            P(("grp", "blk"), None),
            P(("grp", "blk"), None),
            P(None, "blk"),
        ),
        check_vma=False,
    )
```

profile of v0, /device:TPU:0, one launch (start us, length us, event | category | flops | bytes accessed | tf_op | source)
XLA Modules:
  0.0 158.3 jit_solution(8994347896110078273)
XLA Ops:
  7.2 9.0 %all_gather.13 = bf16[512,512]{1,0:T(8,128)(2,1)S(1)} all-gather(bf16[128,512]{1,0:T(8,128)(2,1)} %param.10), channel_id=1, replica_groups=mesh['grp'=8,'blk'=4] {'blk'}, dimensions={0}, use_global_device_ids=true | all-gather | bytes 655360 | tf_op jit(solution)/shard_map/all_gather | solution.py:44
  16.2 1.0 copy.26
  17.2 1.0 copy.24
  18.3 7.5 %all_gather.12 = bf16[512,512]{1,0:T(8,128)(2,1)S(1)} all-gather(bf16[128,512]{1,0:T(8,128)(2,1)} %param.9), channel_id=1, replica_groups=mesh['grp'=8,'blk'=4] {'blk'}, dimensions={0}, use_global_device_ids=true | all-gather | bytes 655360 | tf_op jit(solution)/shard_map/all_gather | solution.py:43
  25.7 1.0 copy.25
  27.5 1.5 fusion.33
  29.0 0.1 fusion.19
  29.1 2.0 %fusion.32 = (f32[128]{0:T(128)S(1)}, f32[8,128,64]{1,2,0:T(8,128)S(1)}) fusion(bf16[512,8,64]{0,2,1:T(8,128)(2,1)} %bitcast.51, f32[8,128,512]{2,1,0:T(8,128)S(1)} %fusion.33, f32[128,512]{1,0:T(8,128)S(1)} %fusion.19), kind=kOutput, calls=%fused_computation.56 | convolution fusion | flops 70844288 | bytes 3146240 | tf_op jit(solution)/shard_map/while/body/eval_jaxpr/hrn,nhd->rhd/dot_general | solution.py:58
  31.3 0.5 add_rsqrt_fusion
  31.9 1.1 copy.27
  33.0 1.6 %fusion.23 = (f32[128]{0:T(128)S(1)}, f32[128]{0:T(128)S(1)}, f32[128,512]{1,0:T(8,128)S(1)}) fusion(f32[512]{0:T(512)S(1)} %copy-done.12, bf16[128,512]{1,0:T(8,128)(2,1)S(1)} %copy-done.9, f32[128]{0:T(128)} %add_rsqrt_fusion, f32[128,512]{1,0:T(8,128)S(1)} %copy.27, f32[128]{0:T(128)S(1)} %broadcast_multiply_fusion.2, bf16[128,1024]{1,0:T(8,128)(2,1)} %param.12, ...), kind=kOutput, calls=%fused_computation.40 | convolution fusion | flops 134741760 | bytes 1970176 | tf_op jit(solution)/shard_map/dot_general | solution.py:70
  34.6 1.8 %multiply_convert_fusion.6 = (bf16[128,512]{1,0:T(8,128)(2,1)}, bf16[128,512]{1,0:T(8,128)(2,1)S(1)}, bf16[128,512]{1,0:T(8,128)(2,1)S(1)}) fusion(f32[128,512]{1,0:T(8,128)S(1)} %get-tuple-element.96, f32[128,512]{1,0:T(8,128)S(1)} %copy.27, f32[512]{0:T(512)S(1)} %copy-done.12, f32[128]{0:T(128)} %add_rsqrt_fusion, f32[128]{0:T(128)S(1)} %broadcast_multiply_fusion.2, ...), kind=kLoop, calls=%fused_computation.28 | loop fusion | flops 983040 | bytes 1052672 | tf_op jit(solution)/shard_map/convert_element_type | solution.py:73
  36.4 0.6 copy-done.1
  37.0 1.8 %fusion.35 = f32[512,1024]{1,0:T(8,128)} fusion(bf16[128,512]{1,0:T(8,128)(2,1)S(1)} %get-tuple-element.93, bf16[128,1024]{1,0:T(8,128)(2,1)S(1)} %copy-done.3), kind=kOutput, calls=%fused_computation.59 | convolution fusion | flops 134217728 | bytes 2490368 | tf_op jit(solution)/shard_map/dot_general | solution.py:82
  38.9 0.8 copy.32
  39.7 0.7 copy.30
  40.6 3.3 %fusion.5 = bf16[8,128,64]{1,2,0:T(8,128)(2,1)} fusion(bf16[512,8,64]{0,2,1:T(8,128)(2,1)} %bitcast.47, f32[8,128,512]{2,1,0:T(8,128)S(1)} %fusion.33, bf16[128,8,64]{0,2,1:T(8,128)(2,1)S(1)} %bitcast.59, bf16[512,8,64]{0,2,1:T(8,128)(2,1)} %bitcast.52, f32[128,512]{1,0:T(8,128)} %copy-done.10), kind=kOutput, calls=%fused_computation.12 | convolution fusion | flops 140115968 | bytes 3670016 | tf_op jit(solution)/shard_map/while/body/eval_jaxpr/hrn,nhd->rhd/dot_general | solution.py:103
  43.9 1.7 %copy.33 = bf16[128,512]{1,0:T(8,128)(2,1)} copy(bf16[128,512]{0,1:T(8,128)(2,1)} %bitcast.58) | data formatting | bytes 262144
  45.6 7.3 %all_gather.15 = bf16[512,512]{1,0:T(8,128)(2,1)S(1)} all-gather(bf16[128,512]{1,0:T(8,128)(2,1)S(1)} %copy-done.7), channel_id=1, replica_groups=mesh['grp'=8,'blk'=4] {'blk'}, dimensions={0}, use_global_device_ids=true | all-gather | bytes 655360 | tf_op jit(solution)/shard_map/all_gather | solution.py:112
  52.8 1.0 copy.31
  53.8 9.5 %all_gather.14 = bf16[512,512]{1,0:T(8,128)(2,1)S(1)} all-gather(bf16[128,512]{1,0:T(8,128)(2,1)S(1)} %get-tuple-element.92), channel_id=1, replica_groups=mesh['grp'=8,'blk'=4] {'blk'}, dimensions={0}, use_global_device_ids=true | all-gather | bytes 655360 | tf_op jit(solution)/shard_map/all_gather | solution.py:113
  63.3 1.0 copy.29
  64.3 0.1 fusion.22
  64.5 1.6 %fusion.34 = f32[8,512,128]{2,1,0:T(8,128)S(1)} fusion(bf16[512,8,64]{0,2,1:T(8,128)(2,1)} %bitcast.48, bf16[128,8,64]{0,2,1:T(8,128)(2,1)S(1)} %bitcast.55), kind=kOutput, calls=%fused_computation.58 | convolution fusion | flops 67108864 | bytes 2752512 | tf_op jit(solution)/shard_map/while/body/eval_jaxpr/nhd,rhd->hnr/dot_general | solution.py:123
  66.2 2.6 %fusion.4 = bf16[8,128,64]{1,2,0:T(8,128)(2,1)S(1)} fusion(bf16[512,8,64]{0,2,1:T(8,128)(2,1)} %bitcast.49, f32[8,512,128]{2,1,0:T(8,128)S(1)} %fusion.34, bf16[512,8,64]{0,2,1:T(8,128)(2,1)} %bitcast.53, bf16[128,8,64]{0,2,1:T(8,128)(2,1)} %bitcast.57, f32[512,128]{1,0:T(8,128)S(1)} %fusion.22), kind=kOutput, calls=%fused_computation.11 | convolution fusion | flops 140115968 | bytes 3670016 | tf_op jit(solution)/shard_map/while/body/eval_jaxpr/hnr,nhd->rhd/dot_general | solution.py:135
  68.8 0.8 copy.34
  69.5 3.2 %reduce-scatter.2.cloned.1.call-done = f32[512,256]{1,0:T(8,128)} async-done(((f32[512,1024]{1,0:T(8,128)}), f32[512,256]{1,0:T(8,128)}) %reduce-scatter.2.cloned.1.call-update) | async-done | bytes 524304 | tf_op jit(solution)/shard_map/reduce_scatter | solution.py:146
  72.7 2.0 %convolution_convert_fusion.1 = bf16[8,64,128]{2,1,0:T(8,128)(2,1)S(1)} fusion(bf16[512,8,64]{0,2,1:T(8,128)(2,1)} %bitcast.54, f32[8,512,128]{2,1,0:T(8,128)S(1)} %fusion.34, f32[512,128]{1,0:T(8,128)} %copy-done.11), kind=kOutput, calls=%fused_computation.13 | convolution fusion | flops 70844416 | bytes 3014656 | tf_op jit(solution)/shard_map/while/body/eval_jaxpr/hnr,nhd->rhd/dot_general | solution.py:138
  74.7 0.8 copy.35
  75.5 1.0 convolution_convert_fusion
  76.5 73.1 %all-reduce.2.cloned.1.call-done = f32[512,256]{1,0:T(8,128)} async-done(((f32[512,256]{1,0:T(8,128)}), f32[512,256]{1,0:T(8,128)}) %all-reduce.2.cloned.1.call-update) | async-done | bytes 524304 | tf_op jit(solution)/shard_map/psum | solution.py:147
  149.6 1.9 %copy.38 = f32[512,256]{1,0:T(8,128)} copy(f32[512,256]{1,0:T(8,128)} %all-reduce.2.cloned.1.call-done) | data formatting | bytes 1048576
  (40 shorter events, 0.5 us)
Async XLA Ops:
  7.2 25.8 %copy-start = (bf16[512,1024]{1,0:T(8,128)(2,1)S(1)}, bf16[512,1024]{1,0:T(8,128)(2,1)}, u32[]{:S(2)}) copy-start(bf16[512,1024]{1,0:T(8,128)(2,1)} %param.15) | copy-start | bytes 3145732
  7.2 65.5 %reduce-scatter.2.cloned.1.call-start = ((), (), s32[]{:S(2)}) async-start(), calls=%async_computation.1 | async-start | bytes 2621440 | tf_op jit(solution)/shard_map/reduce_scatter | solution.py:146
  27.4 3.7 %copy-start.13 = (pred[512]{0:T(512)(128)(4,1)}, pred[512]{0:T(512)(128)(4,1)S(1)}, u32[]{:S(2)}) copy-start(pred[512]{0:T(512)(128)(4,1)S(1)} %iota_compare_fusion.2) | copy-start | bytes 1540
  29.1 2.1 %copy-start.10 = (f32[128,512]{1,0:T(8,128)}, f32[128,512]{1,0:T(8,128)S(1)}, u32[]{:S(2)}) copy-start(f32[128,512]{1,0:T(8,128)S(1)} %fusion.19) | copy-start | bytes 786436
  29.1 3.9 %copy-start.9 = (bf16[128,512]{1,0:T(8,128)(2,1)S(1)}, bf16[128,512]{1,0:T(8,128)(2,1)}, u32[]{:S(2)}) copy-start(bf16[128,512]{1,0:T(8,128)(2,1)} %param.11) | copy-start | bytes 393220
  29.1 3.9 %copy-start.12 = (f32[512]{0:T(512)S(1)}, f32[512]{0:T(512)}, u32[]{:S(2)}) copy-start(f32[512]{0:T(512)} %param.14) | copy-start | bytes 6148
  31.2 0.7 copy-start.4
  33.0 4.0 %copy-start.3 = (bf16[128,1024]{1,0:T(8,128)(2,1)S(1)}, bf16[128,1024]{1,0:T(8,128)(2,1)}, u32[]{:S(2)}) copy-start(bf16[128,1024]{1,0:T(8,128)(2,1)} %param.12) | copy-start | bytes 786436
  36.4 0.6 copy-start.1
  37.0 1.9 %copy-start.5 = (bf16[128,512]{1,0:T(8,128)(2,1)S(1)}, bf16[128,512]{1,0:T(8,128)(2,1)}, u32[]{:S(2)}) copy-start(bf16[128,512]{1,0:T(8,128)(2,1)} %param.9) | copy-start | bytes 393220
  37.0 2.7 %copy-start.6 = (bf16[128,512]{1,0:T(8,128)(2,1)S(1)}, bf16[128,512]{1,0:T(8,128)(2,1)}, u32[]{:S(2)}) copy-start(bf16[128,512]{1,0:T(8,128)(2,1)} %param.10) | copy-start | bytes 393220
  38.9 110.8 %all-reduce.2.cloned.1.call-start = ((), (), s32[]{:S(2)}) async-start(), calls=%async_computation.2 | async-start | bytes 1048576 | tf_op jit(solution)/shard_map/psum | solution.py:147
  40.6 5.0 %copy-start.7 = (bf16[128,512]{1,0:T(8,128)(2,1)S(1)}, bf16[128,512]{1,0:T(8,128)(2,1)}, u32[]{:S(2)}) copy-start(bf16[128,512]{1,0:T(8,128)(2,1)} %param.8) | copy-start | bytes 393220
  43.9 20.5 %copy-start.14 = (pred[512]{0:T(512)(128)(4,1)S(1)}, pred[512]{0:T(512)(128)(4,1)}, u32[]{:S(2)}) copy-start(pred[512]{0:T(512)(128)(4,1)} %copy-done.13) | copy-start | bytes 1540
  43.9 20.6 %copy-start.8 = (bf16[128,512]{0,1:T(8,128)(2,1)S(1)}, bf16[128,512]{0,1:T(8,128)(2,1)}, u32[]{:S(2)}) copy-start(bf16[128,512]{0,1:T(8,128)(2,1)} %copy.32) | copy-start | bytes 393220
  64.5 4.3 %copy-start.11 = (f32[512,128]{1,0:T(8,128)}, f32[512,128]{1,0:T(8,128)S(1)}, u32[]{:S(2)}) copy-start(f32[512,128]{1,0:T(8,128)S(1)} %fusion.22) | copy-start | bytes 786436
  72.7 2.8 %copy-start.2 = (bf16[128,512]{1,0:T(8,128)(2,1)S(1)}, bf16[128,512]{1,0:T(8,128)(2,1)}, u32[]{:S(2)}) copy-start(bf16[128,512]{1,0:T(8,128)(2,1)} %copy-done.1) | copy-start | bytes 393220
Sparse Core Ops, SparseCore 0:
  39.0 33.6 reduce-scatter.1
  76.1 73.4 all-reduce.1
where the time goes:
time: 159 us; the launch traced here: 158 us
  waiting for transfers between devices  76.3 us (48%)
  blocking collectives  33.2 us (21%)
  matrix products  17.5 us (11%)
  between operations  14.9 us (9%)
  local copies, waits for them, and re-layouts  13.7 us (9%)
  other arithmetic  2.64 us (2%)
    psum x1, waiting for transfers between devices, shards(): grad_weight = lax.psum(column_part, 'grp')  73.1 us
    all_gather x1, blocking collectives, shards(): grad_piece = lax.all_gather(attended_grad, 'blk', axis=0, tiled=True)  9.49 us
    all_gather x1, blocking collectives, shards(): lax.all_gather(value, 'blk', axis=0, tiled=True)  8.99 us
    unnamed x37, local copies, waits for them, and re-layouts  8.42 us
    all_gather x1, blocking collectives, shards(): lax.all_gather(key, 'blk', axis=0, tiled=True)  7.49 us
    all_gather x1, blocking collectives, shards(): query_piece = lax.all_gather(query, 'blk', axis=0, tiled=True)  7.27 us
    dot_general x1, matrix products, query_step(): jnp.einsum('hrn,nhd->rhd', score_grad, key_block, preferred_element_type=...  3.29 us
  transfers between devices with their start and end apart: 2, of which 2 were waited for; matrix products, arithmetic and copies ran while one was open for 11% of the time, Pallas kernels for 0%

commit v1 on v0

--- a/solution.py
+++ b/solution.py
@@ -144,7 +144,7 @@
     grad_key = (key_acc * scale).reshape(rows, HEADS * HEAD).astype(jnp.bfloat16)
     grad_value = value_acc.reshape(rows, HEADS * HEAD).astype(jnp.bfloat16)
     column_part = lax.psum_scatter(weight_term, "blk", scatter_dimension=1, tiled=True)
-    grad_weight = lax.psum(column_part, "grp")
+    grad_weight = jnp.sum(lax.all_gather(column_part, "grp"), axis=0)
     return (layer_out, grad_query, grad_key, grad_value, grad_gate, grad_weight)
 
 

time: 159 us -> 149 us (0.937)
  local copies, waits for them, and re-layouts: 13.7 us -> 6.69 us
  matrix products: 17.5 us -> 12.8 us
  blocking collectives: 33.2 us -> 30.2 us
  waiting for transfers between devices: 76.3 us -> 79.2 us
  other arithmetic: 2.64 us -> 4.52 us
    psum x1 -> x0, waiting for transfers between devices: 73.1 us -> none  [shards(): grad_weight = lax.psum(column_part, 'grp')]
    all_gather x0 -> x1, waiting for transfers between devices: none -> 47 us  [shards(): grad_weight = jnp.sum(lax.all_gather(column_part, 'grp'), axis=0)]
    reduce_scatter x1, waiting for transfers between devices: 3.17 us -> 32.1 us  [shards(): lax.psum_scatter(weight_term, 'blk', scatter_dimension=1, tiled=True)]
    unnamed x37 -> x28, local copies, waits for them, and re-layouts: 8.42 us -> 3.99 us
    reduce_sum x0 -> x1, other arithmetic: none -> 3.31 us  [shards(): grad_weight = jnp.sum(lax.all_gather(column_part, 'grp'), axis=0)]
    all_gather x1, blocking collectives: 9.49 us -> 7.27 us  [shards(): grad_piece = lax.all_gather(attended_grad, 'blk', axis=0, tiled=True)]
  transfers between devices with their start and end apart: 2 -> 2, of which waited for: 2 -> 2; matrix products, arithmetic and copies ran while one was open for 11% -> 9% of each run, Pallas kernels for 0% -> 0%
where the time goes in v1:
time: 149 us
  waiting for transfers between devices  79.2 us (53%)
  blocking collectives  30.2 us (20%)
  between operations  15 us (10%)
  matrix products  12.8 us (9%)
  local copies, waits for them, and re-layouts  6.69 us (4%)
  other arithmetic  4.52 us (3%)
    all_gather x1, waiting for transfers between devices, shards(): grad_weight = jnp.sum(lax.all_gather(column_part, 'grp'), axis=0)  47 us
    reduce_scatter x1, waiting for transfers between devices, shards(): lax.psum_scatter(weight_term, 'blk', scatter_dimension=1, tiled=True)  32.1 us
    all_gather x1, blocking collectives, shards(): lax.all_gather(key, 'blk', axis=0, tiled=True)  8.86 us
    all_gather x1, blocking collectives, shards(): lax.all_gather(value, 'blk', axis=0, tiled=True)  7.49 us
    all_gather x1, blocking collectives, shards(): grad_piece = lax.all_gather(attended_grad, 'blk', axis=0, tiled=True)  7.27 us
    all_gather x1, blocking collectives, shards(): query_piece = lax.all_gather(query, 'blk', axis=0, tiled=True)  6.61 us
    unnamed x28, local copies, waits for them, and re-layouts  3.99 us
    reduce_sum x1, other arithmetic, shards(): grad_weight = jnp.sum(lax.all_gather(column_part, 'grp'), axis=0)  3.31 us
  transfers between devices with their start and end apart: 2, of which 2 were waited for; matrix products, arithmetic and copies ran while one was open for 9% of the time, Pallas kernels for 0%

profile of v1, /device:TPU:0, one launch (start us, length us, event | category | flops | bytes accessed | tf_op | source)
XLA Modules:
  0.0 148.5 jit_solution(10595568718587752208)
XLA Ops:
  8.0 1.0 copy.24
  9.0 8.9 %all_gather.18 = bf16[512,512]{1,0:T(8,128)(2,1)S(1)} all-gather(bf16[128,512]{1,0:T(8,128)(2,1)} %param.9), channel_id=1, replica_groups=mesh['grp'=8,'blk'=4] {'blk'}, dimensions={0}, use_global_device_ids=true | all-gather | bytes 655360 | tf_op jit(solution)/shard_map/all_gather | solution.py:43
  17.9 0.2 copy.25
  18.1 7.5 %all_gather.19 = bf16[512,512]{1,0:T(8,128)(2,1)S(1)} all-gather(bf16[128,512]{1,0:T(8,128)(2,1)} %param.10), channel_id=1, replica_groups=mesh['grp'=8,'blk'=4] {'blk'}, dimensions={0}, use_global_device_ids=true | all-gather | bytes 655360 | tf_op jit(solution)/shard_map/all_gather | solution.py:44
  25.6 0.2 copy.26
  25.8 0.5 fusion.33
  26.3 0.1 fusion.19
  26.5 0.8 fusion.32
  27.3 0.3 copy-done.1
  27.8 0.1 copy.27
  28.0 0.6 fusion.23
  28.6 0.8 multiply_convert_fusion.6
  29.4 1.8 %fusion.35 = f32[512,1024]{1,0:T(8,128)} fusion(bf16[128,512]{1,0:T(8,128)(2,1)S(1)} %get-tuple-element.93, bf16[128,1024]{1,0:T(8,128)(2,1)S(1)} %copy-done.2), kind=kOutput, calls=%fused_computation.59 | convolution fusion | flops 134217728 | bytes 2490368 | tf_op jit(solution)/shard_map/dot_general | solution.py:82
  31.3 32.1 %reduce-scatter.2.cloned.1.call-done = f32[512,256]{1,0:T(8,128)} async-done(((f32[512,1024]{1,0:T(8,128)}), f32[512,256]{1,0:T(8,128)}) %reduce-scatter.2.cloned.1.call-update) | async-done | bytes 524304 | tf_op jit(solution)/shard_map/reduce_scatter | solution.py:146
  63.4 0.1 copy.32
  63.5 0.1 copy.30
  63.7 6.6 %all_gather.21 = bf16[512,512]{1,0:T(8,128)(2,1)S(1)} all-gather(bf16[128,512]{1,0:T(8,128)(2,1)S(1)} %copy-done.5), channel_id=1, replica_groups=mesh['grp'=8,'blk'=4] {'blk'}, dimensions={0}, use_global_device_ids=true | all-gather | bytes 655360 | tf_op jit(solution)/shard_map/all_gather | solution.py:112
  70.3 1.0 copy.31
  71.3 0.1 copy.28
  71.4 3.0 %fusion.5 = bf16[8,128,64]{1,2,0:T(8,128)(2,1)S(1)} fusion(bf16[512,8,64]{0,2,1:T(8,128)(2,1)S(1)} %bitcast.49, f32[8,128,512]{2,1,0:T(8,128)} %copy-done.1, bf16[128,8,64]{0,2,1:T(8,128)(2,1)S(1)} %bitcast.62, bf16[512,8,64]{0,2,1:T(8,128)(2,1)S(1)} %bitcast.54, f32[128,512]{1,0:T(8,128)} %copy-done.8), kind=kOutput, calls=%fused_computation.12 | convolution fusion | flops 140115968 | bytes 3670016 | tf_op jit(solution)/shard_map/while/body/eval_jaxpr/hrn,nhd->rhd/dot_general | solution.py:103
  74.4 0.8 copy.33
  75.2 7.3 %all_gather.20 = bf16[512,512]{1,0:T(8,128)(2,1)S(1)} all-gather(bf16[128,512]{1,0:T(8,128)(2,1)S(1)} %get-tuple-element.92), channel_id=1, replica_groups=mesh['grp'=8,'blk'=4] {'blk'}, dimensions={0}, use_global_device_ids=true | all-gather | bytes 655360 | tf_op jit(solution)/shard_map/all_gather | solution.py:113
  82.5 1.0 copy.29
  83.5 0.1 fusion.22
  83.6 1.7 %fusion.34 = f32[8,512,128]{2,1,0:T(8,128)S(1)} fusion(bf16[512,8,64]{0,2,1:T(8,128)(2,1)} %bitcast.50, bf16[128,8,64]{0,2,1:T(8,128)(2,1)S(1)} %bitcast.57), kind=kOutput, calls=%fused_computation.58 | convolution fusion | flops 67108864 | bytes 2752512 | tf_op jit(solution)/shard_map/while/body/eval_jaxpr/nhd,rhd->hnr/dot_general | solution.py:123
  85.3 0.8 convolution_convert_fusion.1
  86.2 0.8 copy.35
  86.9 2.6 %fusion.4 = bf16[8,128,64]{1,2,0:T(8,128)(2,1)S(1)} fusion(bf16[512,8,64]{0,2,1:T(8,128)(2,1)} %bitcast.51, f32[8,512,128]{2,1,0:T(8,128)S(1)} %fusion.34, bf16[512,8,64]{0,2,1:T(8,128)(2,1)} %bitcast.55, bf16[128,8,64]{0,2,1:T(8,128)(2,1)S(1)} %bitcast.59, f32[512,128]{1,0:T(8,128)} %copy-done.9), kind=kOutput, calls=%fused_computation.11 | convolution fusion | flops 140115968 | bytes 3670016 | tf_op jit(solution)/shard_map/while/body/eval_jaxpr/hnr,nhd->rhd/dot_general | solution.py:135
  89.6 0.8 copy.34
  90.3 1.0 convolution_convert_fusion
  91.3 47.0 %all-gather.3.cloned.1.call-done = f32[4096,256]{1,0:T(8,128)} async-done(((f32[512,256]{1,0:T(8,128)}), f32[4096,256]{1,0:T(8,128)}) %all-gather.3.cloned.1.call-update) | async-done | bytes 4194320 | tf_op jit(solution)/shard_map/all_gather | solution.py:147
  138.4 3.3 %reduce_sum.49 = f32[512,256]{1,0:T(8,128)} reduce(f32[8,512,256]{2,1,0:T(8,128)} %bitcast.47, f32[]{:T(128)} %constant.45.clone.1), dimensions={0}, to_apply=%region_5.6 | reduce | flops 917504 | bytes 4718596 | tf_op jit(solution)/shard_map/reduce_sum | solution.py:147
  (32 shorter events, 0.4 us)
Async XLA Ops:
  7.2 20.8 %copy-start = (bf16[512,1024]{1,0:T(8,128)(2,1)S(1)}, bf16[512,1024]{1,0:T(8,128)(2,1)}, u32[]{:S(2)}) copy-start(bf16[512,1024]{1,0:T(8,128)(2,1)} %param.15) | copy-start | bytes 3145732
  7.2 56.2 %reduce-scatter.2.cloned.1.call-start = ((), (), s32[]{:S(2)}) async-start(), calls=%async_computation.1 | async-start | bytes 2621440 | tf_op jit(solution)/shard_map/reduce_scatter | solution.py:146
  26.3 1.3 copy-start.1
  26.4 1.3 copy-start.8
  26.4 1.5 %copy-start.2 = (bf16[128,1024]{1,0:T(8,128)(2,1)S(1)}, bf16[128,1024]{1,0:T(8,128)(2,1)}, u32[]{:S(2)}) copy-start(bf16[128,1024]{1,0:T(8,128)(2,1)} %param.12) | copy-start | bytes 786436
  26.5 1.5 %copy-start.7 = (bf16[128,512]{1,0:T(8,128)(2,1)S(1)}, bf16[128,512]{1,0:T(8,128)(2,1)}, u32[]{:S(2)}) copy-start(bf16[128,512]{1,0:T(8,128)(2,1)} %param.11) | copy-start | bytes 393220
  26.5 1.5 %copy-start.10 = (f32[512]{0:T(512)S(1)}, f32[512]{0:T(512)}, u32[]{:S(2)}) copy-start(f32[512]{0:T(512)} %param.14) | copy-start | bytes 6148
  29.4 34.0 %copy-start.3 = (bf16[128,512]{1,0:T(8,128)(2,1)S(1)}, bf16[128,512]{1,0:T(8,128)(2,1)}, u32[]{:S(2)}) copy-start(bf16[128,512]{1,0:T(8,128)(2,1)} %param.9) | copy-start | bytes 393220
  29.4 34.1 %copy-start.4 = (bf16[128,512]{1,0:T(8,128)(2,1)S(1)}, bf16[128,512]{1,0:T(8,128)(2,1)}, u32[]{:S(2)}) copy-start(bf16[128,512]{1,0:T(8,128)(2,1)} %param.10) | copy-start | bytes 393220
  31.2 32.5 %copy-start.5 = (bf16[128,512]{1,0:T(8,128)(2,1)S(1)}, bf16[128,512]{1,0:T(8,128)(2,1)}, u32[]{:S(2)}) copy-start(bf16[128,512]{1,0:T(8,128)(2,1)} %param.8) | copy-start | bytes 393220
  31.2 107.1 %all-gather.3.cloned.1.call-start = ((), (), s32[]{:S(2)}) async-start(), calls=%async_computation.2 | async-start | bytes 4718592 | tf_op jit(solution)/shard_map/all_gather | solution.py:147
  83.5 1.8 %copy-start.6 = (bf16[512,512]{0,1:T(8,128)(2,1)S(1)}, bf16[512,512]{0,1:T(8,128)(2,1)}, u32[]{:S(2)}) copy-start(bf16[512,512]{0,1:T(8,128)(2,1)} %copy.29) | copy-start | bytes 1572868
  83.6 2.5 %copy-start.9 = (f32[512,128]{1,0:T(8,128)}, f32[512,128]{1,0:T(8,128)S(1)}, u32[]{:S(2)}) copy-start(f32[512,128]{1,0:T(8,128)S(1)} %fusion.22) | copy-start | bytes 786436
Sparse Core Ops, SparseCore 0:
  31.3 31.9 reduce-scatter.1
  65.5 72.8 all-gather.2
